TPU v7x, 32 devices: a whole 2x2x4 slice. The times are simulated.
32 devices in a mesh: ga: 8 (over z, y), band: 4 (over x, core).
Axes of the slice: x: 2, y: 2, z: 4, core: 2. Of those that a mesh axis runs over, the one named last changes fastest.
Arguments:
- coeffs: bfloat16 [2048, 128], P('ga', 'band'), may hold values from -6 to 6
- coupling: bfloat16 [12288, 12288], P('ga', 'band'), may hold values from -0.21875 to 0.21875
- miller: int32 [3, 2048], P(None, 'ga'), may hold values from -24 to 24
- species: int32 [1024], replicated, may hold values from 0 to 3
- proj_atom: int32 [12288], replicated, may hold values from 0 to 1023, as said below
- positions: float32 [3, 1024], replicated, may hold values from 0 to 1
- radial: float32 [12, 128], replicated, may hold values from -8 to 8
Outputs:
- result: bfloat16 [2048, 128], P('ga', 'band')
Inputs may be any that keep to these rules, and one draw needn't show every extreme that they name: `proj_atom`: projector p has channel p mod 12; each atom owns 12 consecutive projectors.
All inputs are finite; a program needn't handle non-finite values.
Results may differ from a plain program's by a relative error of at most 0.008.
Values may be sent and summed in bfloat16 or wider, within the bound.
No kernel may reach another device: no remote copies, remote signals or barrier semaphores. Data moves between devices by JAX's collectives and lax.ppermute only.
A program may use at most 128 MiB of HBM per device.

v0:
```python
import math
import jax
import jax.numpy as jnp
from jax import lax
from jax.sharding import PartitionSpec as P

NCH = 12
SHELLS = 3
KINDS = 4
QBINS = 128
MMAX = 24
NPROJ = 12288


def radial_values(miller_block, radial):
    mf = miller_block.astype(jnp.float32)
    qval = (mf[0] * mf[0] + mf[1] * mf[1] + mf[2] * mf[2]) * ((QBINS - 1) / (3.0 * MMAX * MMAX))
    knots = jnp.arange(QBINS, dtype=jnp.int32).astype(jnp.float32)
    hats = jnp.maximum(0.0, 1.0 - jnp.abs(qval[:, None] - knots[None, :]))
    return jnp.dot(hats, radial.T, precision=lax.Precision.HIGHEST)


def beta_columns(miller_block, radval, species, proj_atom, positions, start, count, scale):
    mf = miller_block.astype(jnp.float32)
    atoms = lax.dynamic_slice_in_dim(proj_atom, jnp.asarray(start).astype(jnp.int32), count)
    channel = (jnp.asarray(start).astype(jnp.int32) + jnp.arange(count, dtype=jnp.int32)) % NCH
    shell = channel // 4
    comp = channel % 4
    kind = jnp.take(species, atoms)
    column = kind * SHELLS + shell
    select = (column[None, :] == jnp.arange(KINDS * SHELLS, dtype=jnp.int32)[:, None]).astype(
        jnp.float32
    )
    radpart = jnp.dot(radval, select, precision=lax.Precision.HIGHEST)
    place = jnp.take(positions, atoms, axis=1)
    theta = (
        2.0
        * math.pi
        * (
            mf[0][:, None] * place[0][None, :]
            + mf[1][:, None] * place[1][None, :]
            + mf[2][:, None] * place[2][None, :]
        )
    )
    unit = mf / MMAX
    angular = jnp.where(
        comp[None, :] == 1,
        unit[0][:, None],
        jnp.where(
            comp[None, :] == 2,
            unit[1][:, None],
            jnp.where(comp[None, :] == 3, unit[2][:, None], jnp.ones_like(theta)),
        ),
    )
    phase = jnp.where(comp[None, :] == 0, jnp.cos(theta), jnp.sin(theta))
    return (radpart * angular * phase * scale).astype(jnp.bfloat16)


def beta_atoms(miller_block, radval, species, proj_atom, positions, start, count, scale):
    mf = miller_block.astype(jnp.float32)
    npw = mf.shape[1]
    natoms = count // NCH
    owners = lax.dynamic_slice_in_dim(proj_atom, jnp.asarray(start).astype(jnp.int32), count)
    atoms = owners.reshape(natoms, NCH)[:, 0]
    kind = jnp.take(species, atoms)
    column = kind[:, None] * SHELLS + jnp.arange(SHELLS, dtype=jnp.int32)[None, :]
    select = (
        column.reshape(-1)[None, :] == jnp.arange(KINDS * SHELLS, dtype=jnp.int32)[:, None]
    ).astype(jnp.float32)
    radpart = jnp.dot(radval, select, precision=lax.Precision.HIGHEST).reshape(npw, natoms, SHELLS)
    place = jnp.take(positions, atoms, axis=1)
    theta = (
        2.0
        * math.pi
        * (
            mf[0][:, None] * place[0][None, :]
            + mf[1][:, None] * place[1][None, :]
            + mf[2][:, None] * place[2][None, :]
        )
    )
    cosine = jnp.cos(theta)
    sine = jnp.sin(theta)
    unit = mf / MMAX
    ones = jnp.ones((npw, natoms), jnp.float32)
    angular = jnp.stack(
        [
            ones,
            jnp.broadcast_to(unit[0][:, None], (npw, natoms)),
            jnp.broadcast_to(unit[1][:, None], (npw, natoms)),
            jnp.broadcast_to(unit[2][:, None], (npw, natoms)),
        ],
        axis=2,
    )
    phase = jnp.stack([cosine, sine, sine, sine], axis=2)
    values = radpart[:, :, :, None] * angular[:, :, None, :] * phase[:, :, None, :] * scale
    return values.reshape(npw, count).astype(jnp.bfloat16)


def make_beta(miller_block, radval, species, proj_atom, positions, start, count, scale, aligned):
    if aligned and count % NCH == 0:
        return beta_atoms(miller_block, radval, species, proj_atom, positions, start, count, scale)
    return beta_columns(miller_block, radval, species, proj_atom, positions, start, count, scale)


def block_size(count):
    width = 1
    for cand in range(min(count, 768), 0, -1):
        if count % cand == 0:
            width = cand
            break
    return width


def shards(coeffs, coupling, miller, species, proj_atom, positions, radial):
    scale = 1.0 / math.sqrt(coeffs.shape[0] * lax.axis_size("ga"))
    radval = radial_values(miller, radial)
    nbands = coeffs.shape[1]
    aligned = coupling.shape[0] % NCH == 0
    width = block_size(NPROJ)
    starts = width * jnp.arange(NPROJ // width, dtype=jnp.int32)

    def one_block(first):
        beta = make_beta(
            miller, radval, species, proj_atom, positions, first, width, scale, aligned
        )
        return lax.dot_general(
            beta, coeffs, (((0,), (0,)), ((), ())), preferred_element_type=jnp.float32
        )

    summed = lax.psum(lax.map(one_block, starts).reshape(NPROJ, nbands), "ga")
    proj_b = summed.astype(jnp.bfloat16)
    full_rows = lax.all_gather(coupling, "band", axis=1, tiled=True)
    mixed = jnp.dot(full_rows, proj_b, preferred_element_type=jnp.float32).astype(jnp.bfloat16)
    piece = jax.tree.map(lambda part: lax.all_gather(part, "ga", axis=0, tiled=True), mixed)
    start = jnp.int32(0)
    count = piece.shape[0]
    add_width = block_size(count)

    def step(index, acc):
        first = start + index * add_width
        beta = make_beta(
            miller, radval, species, proj_atom, positions, first, add_width, scale, aligned
        )
        rows = lax.dynamic_slice_in_dim(piece, index * add_width, add_width, 0)
        return acc + jnp.dot(beta, rows, preferred_element_type=jnp.float32)

    summed_back = lax.fori_loop(0, count // add_width, step, coeffs.astype(jnp.float32))
    return summed_back.astype(jnp.bfloat16)


def solution(mesh):
    placed = (P("ga", "band"), P("ga", "band"), P(None, "ga"), P(), P(), P(), P())
    return jax.shard_map(
        shards, mesh=mesh, in_specs=placed, out_specs=P("ga", "band"), check_vma=False
    )
```

profile of v0, /device:TPU:0, one launch (start us, length us, event | category | flops | bytes accessed | tf_op | source)
XLA Modules:
  0.0 415.7 jit_solution(7675885683890201779)
XLA Ops:
  7.9 172.2 %while.27 = (s32[]{:T(128)}, f32[16,768,32]{1,0,2:T(8,128)S(1)}, s32[16]{0:T(128)S(1)}, s32[12288]{0:T(1024)}, s32[1024]{0:T(1024)S(1)}, /*index=5*/f32[256,12]{...) while((s32[]{:T(128)}, f32[16,768,32]{1,0,2:T(8,128)S(1)}, ...), condition=%wide.region_1.4_spmd, body=%wide.region_0.3_spmd.sunk | while | flops 20943940 | bytes 5160803 | solution.py:130
  15.5 3.2 dynamic_update_slice.7
  26.3 3.2 dynamic_update_slice.7
  37.1 3.2 dynamic_update_slice.7
  47.8 3.2 dynamic_update_slice.7
  58.6 3.2 dynamic_update_slice.7
  69.3 3.2 dynamic_update_slice.7
  80.1 3.2 dynamic_update_slice.7
  90.9 3.2 dynamic_update_slice.7
  101.6 3.2 dynamic_update_slice.7
  112.4 3.2 dynamic_update_slice.7
  123.2 3.2 dynamic_update_slice.7
  133.9 3.2 dynamic_update_slice.7
  144.7 3.2 dynamic_update_slice.7
  155.5 3.2 dynamic_update_slice.7
  166.2 3.2 dynamic_update_slice.7
  177.0 3.2 dynamic_update_slice.7
  181.9 83.1 %all-reduce.1 = bf16[12288,32]{0,1:T(8,128)(2,1)S(1)} all-reduce(f32[12288,32]{0,1:T(8,128)S(1)} %bitcast.98), channel_id=1, replica_groups=mesh['ga'=8,'band'=4] {'ga'}, use_global_device_ids=true, to_apply=%region_2.0 | all-reduce | flops 393216 | bytes 2359296 | tf_op jit(solution)/shard_map/psum | solution.py:130
  265.0 16.8 %fusion.8 = bf16[1536,32]{0,1:T(8,128)(2,1)S(1)} fusion(bf16[1536,12288]{1,0:T(8,128)(2,1)} %all-gather.2.cloned.1.call-done, bf16[12288,32]{0,1:T(8,128)(2,1)S(1)} %all-reduce.1), kind=kOutput, calls=%fused_computation.49 | convolution fusion | flops 1208008704 | bytes 38633472 | tf_op jit(solution)/shard_map/dot_general | solution.py:133
  281.9 31.7 %all_gather.7 = bf16[12288,32]{0,1:T(8,128)(2,1)S(1)} all-gather(bf16[1536,32]{0,1:T(8,128)(2,1)S(1)} %fusion.8), channel_id=1, replica_groups=mesh['ga'=8,'band'=4] {'ga'}, dimensions={0}, use_global_device_ids=true | all-gather | bytes 884736 | tf_op jit(solution)/shard_map/all_gather | solution.py:134
  313.5 94.7 %while.28 = (s32[]{:T(128)}, f32[256,32]{0,1:T(8,128)S(1)}, s32[12288]{0:T(1024)}, s32[1024]{0:T(1024)S(1)}, f32[256,12]{0,1:T(8,128)S(1)}, /*index=5*/f32[3,256...) while((s32[]{:T(128)}, f32[256,32]{0,1:T(8,128)S(1)}, ...), condition=%wide.region_4.7_spmd, body=%wide.region_3.6_spmd.sunk | while | flops 20952132 | bytes 4767587 | solution.py:147
  321.2 1.6 gather_fusion.2
  344.9 1.6 gather_fusion.2
  350.8 1.6 gather_fusion.2
  (950 shorter events, 179.0 us)
Async XLA Ops:
  6.5 1.1 copy-start
  6.5 0.8 copy-start.5
  6.5 0.8 copy-start.4
  6.5 1.0 copy-start.3
  6.5 1.4 copy-start.1
  6.5 258.5 %all-gather.2.cloned.1.call-start = ((), (), s32[]{:S(2)}) async-start(), calls=%async_computation | async-start | bytes 47185920 | tf_op jit(solution)/shard_map/all_gather | solution.py:132
  180.2 0.8 copy-start.2
Sparse Core Ops, SparseCore 0:
  8.9 229.8 all-gather.1
where the time goes:
time: 418 us; the launch traced here: 416 us
  local copies, waits for them, and re-layouts  181 us (43%)
  blocking collectives  115 us (28%)
  other arithmetic  37.1 us (9%)
  loops' own time  35.3 us (8%)
  matrix products  33.3 us (8%)
  between operations  13.6 us (3%)
    psum x1, blocking collectives, shards(): summed = lax.psum(lax.map(one_block, starts).reshape(NPROJ, nbands), 'ga')  83.1 us
    dynamic_update_slice x32, local copies, waits for them, and re-layouts, shards(): summed = lax.psum(lax.map(one_block, starts).reshape(NPROJ, nbands), 'ga')  53.2 us
    gather x32, local copies, waits for them, and re-layouts, beta_atoms(): place = jnp.take(positions, atoms, axis=1)  35.9 us
    another operation x1, loops' own time, shards(): summed = lax.psum(lax.map(one_block, starts).reshape(NPROJ, nbands), 'ga')  32.7 us
    all_gather x1, blocking collectives, shards(): lax.all_gather(part, 'ga', axis=0, tiled=True)  31.7 us
    dynamic_slice x32, local copies, waits for them, and re-layouts, beta_atoms(): lax.dynamic_slice_in_dim(proj_atom, jnp.asarray(start).astype(jnp.int32),...  25 us
    gather x32, local copies, waits for them, and re-layouts, beta_atoms(): kind = jnp.take(species, atoms)  23.3 us
    dot_general x1, matrix products, shards(): jnp.dot(full_rows, proj_b, preferred_element_type=jnp.float32)  16.8 us
  transfers between devices with their start and end apart: 1, of which 0 were waited for; matrix products, arithmetic and copies ran while one was open for 34% of the time, Pallas kernels for 0%

commit v1 on v0

--- a/solution.py
+++ b/solution.py
@@ -127,7 +127,9 @@
             beta, coeffs, (((0,), (0,)), ((), ())), preferred_element_type=jnp.float32
         )
 
-    summed = lax.psum(lax.map(one_block, starts).reshape(NPROJ, nbands), "ga")
+    summed = jnp.sum(
+        lax.all_gather(lax.map(one_block, starts).reshape(NPROJ, nbands), "ga"), axis=0
+    )
     proj_b = summed.astype(jnp.bfloat16)
     full_rows = lax.all_gather(coupling, "band", axis=1, tiled=True)
     mixed = jnp.dot(full_rows, proj_b, preferred_element_type=jnp.float32).astype(jnp.bfloat16)

time: 418 us -> 755 us (1.81)
  waiting for transfers between devices: 0.7 us -> 400 us
  blocking collectives: 115 us -> 32.3 us
  matrix products: 33.3 us -> 44.7 us
    all_gather x1, waiting for transfers between devices: 0.02 us -> 222 us  [shards(): full_rows = lax.all_gather(coupling, 'band', axis=1, tiled=True)]
    all_gather x0 -> x1, waiting for transfers between devices: none -> 178 us  [shards(): lax.all_gather(lax.map(one_block, starts).reshape(NPROJ, nbands), 'ga')]
    psum x1 -> x0, blocking collectives: 83.1 us -> none  [shards(): summed = lax.psum(lax.map(one_block, starts).reshape(NPROJ, nbands), 'ga')]
    gather x32, local copies, waits for them, and re-layouts: 35.9 us -> 19.2 us  [beta_atoms(): place = jnp.take(positions, atoms, axis=1)]
    gather x32, local copies, waits for them, and re-layouts: 23.3 us -> 35.1 us  [beta_atoms(): kind = jnp.take(species, atoms)]
    dot_general x16, matrix products: 3.87 us -> 15.3 us  [one_block(): lax.dot_general(beta, coeffs, (((0,), (0,)), ((), ())), preferred_element...]
  transfers between devices with their start and end apart: 1 -> 2, of which waited for: 0 -> 2; matrix products, arithmetic and copies ran while one was open for 34% -> 1% of each run, Pallas kernels for 0% -> 0%
where the time goes in v1:
time: 755 us; the launch traced here: 750 us
  waiting for transfers between devices  400 us (53%)
  local copies, waits for them, and re-layouts  178 us (24%)
  matrix products  44.7 us (6%)
  other arithmetic  43.1 us (6%)
  loops' own time  38.5 us (5%)
  blocking collectives  32.3 us (4%)
  between operations  13.5 us (2%)
    all_gather x1, waiting for transfers between devices, shards(): full_rows = lax.all_gather(coupling, 'band', axis=1, tiled=True)  222 us
    all_gather x1, waiting for transfers between devices, shards(): lax.all_gather(lax.map(one_block, starts).reshape(NPROJ, nbands), 'ga')  178 us
    dynamic_update_slice x32, local copies, waits for them, and re-layouts, shards(): lax.map(one_block, starts).reshape(NPROJ, nbands)  53.3 us
    another operation x1, loops' own time, shards(): lax.map(one_block, starts).reshape(NPROJ, nbands)  35.9 us
    gather x32, local copies, waits for them, and re-layouts, beta_atoms(): kind = jnp.take(species, atoms)  35.1 us
    all_gather x1, blocking collectives, shards(): lax.all_gather(part, 'ga', axis=0, tiled=True)  32.3 us
    dynamic_slice x32, local copies, waits for them, and re-layouts, beta_atoms(): lax.dynamic_slice_in_dim(proj_atom, jnp.asarray(start).astype(jnp.int32),...  25 us
    gather x32, local copies, waits for them, and re-layouts, beta_atoms(): place = jnp.take(positions, atoms, axis=1)  19.2 us
  transfers between devices with their start and end apart: 2, of which 2 were waited for; matrix products, arithmetic and copies ran while one was open for 1% of the time, Pallas kernels for 0%

profile of v1, /device:TPU:0, one launch (start us, length us, event | category | flops | bytes accessed | tf_op | source)
XLA Modules:
  0.0 750.3 jit_solution(11048882218585078548)
XLA Ops:
  8.5 199.7 %while.27 = (s32[]{:T(128)}, f32[16,768,32]{1,0,2:T(8,128)S(1)}, s32[16]{0:T(128)S(1)}, s32[12288]{0:T(1024)}, s32[1024]{0:T(1024)}, /*index=5*/f32[256,12]{0,1:...) while((s32[]{:T(128)}, f32[16,768,32]{1,0,2:T(8,128)S(1)}, ...), condition=%wide.region_1.4_spmd, body=%wide.region_0.3_spmd.sunk | while | flops 20943940 | bytes 5160803 | solution.py:131
  12.3 1.5 gather_fusion.1
  17.8 3.2 dynamic_update_slice.7
  30.3 3.2 dynamic_update_slice.7
  42.7 3.2 dynamic_update_slice.7
  55.2 3.2 dynamic_update_slice.7
  67.7 3.2 dynamic_update_slice.7
  80.2 3.2 dynamic_update_slice.7
  92.7 3.2 dynamic_update_slice.7
  105.1 3.2 dynamic_update_slice.7
  117.6 3.2 dynamic_update_slice.7
  130.1 3.2 dynamic_update_slice.7
  142.6 3.2 dynamic_update_slice.7
  155.1 3.2 dynamic_update_slice.7
  167.5 3.2 dynamic_update_slice.7
  180.0 3.2 dynamic_update_slice.7
  192.5 3.2 dynamic_update_slice.7
  205.0 3.2 dynamic_update_slice.7
  210.4 178.2 %all-gather.3.cloned.1.call-done = f32[8,12288,32]{1,2,0:T(8,128)} async-done(((f32[1,12288,32]{1,2,0:T(8,128)}), f32[8,12288,32]{1,2,0:T(8,128)}) %all-gather.3.cloned.1.call-update) | async-done | bytes 12582928 | tf_op jit(solution)/shard_map/all_gather | solution.py:131
  388.6 5.4 reduce_sum.9
  394.0 221.6 %all-gather.5.cloned.1.call-done = bf16[1536,12288]{1,0:T(8,128)(2,1)} async-done(((bf16[1536,3072]{1,0:T(8,128)(2,1)}), bf16[1536,12288]{1,0:T(8,128)(2,1)}) %all-gather.5.cloned.1.call-update) | async-done | bytes 37748752 | tf_op jit(solution)/shard_map/all_gather | solution.py:134
  615.6 16.8 %fusion.8 = bf16[1536,32]{0,1:T(8,128)(2,1)S(1)} fusion(bf16[1536,12288]{1,0:T(8,128)(2,1)} %all-gather.5.cloned.1.call-done, bf16[12288,32]{0,1:T(8,128)(2,1)S(1)} %reduce_sum.9), kind=kOutput, calls=%fused_computation.49 | convolution fusion | flops 1208008704 | bytes 38633472 | tf_op jit(solution)/shard_map/dot_general | solution.py:135
  632.4 32.3 %all_gather.11 = bf16[12288,32]{0,1:T(8,128)(2,1)S(1)} all-gather(bf16[1536,32]{0,1:T(8,128)(2,1)S(1)} %fusion.8), channel_id=1, replica_groups=mesh['ga'=8,'band'=4] {'ga'}, dimensions={0}, use_global_device_ids=true | all-gather | bytes 884736 | tf_op jit(solution)/shard_map/all_gather | solution.py:136
  664.7 78.1 %while.28 = (s32[]{:T(128)}, f32[256,32]{0,1:T(8,128)S(1)}, s32[12288]{0:T(1024)}, s32[1024]{0:T(1024)S(1)}, f32[256,12]{0,1:T(8,128)S(1)}, /*index=5*/f32[3,256...) while((s32[]{:T(128)}, f32[256,32]{0,1:T(8,128)S(1)}, ...), condition=%wide.region_4.7_spmd, body=%wide.region_3.6_spmd.sunk | while | flops 20952132 | bytes 4767587 | solution.py:149
  (949 shorter events, 191.2 us)
Async XLA Ops:
  6.5 1.7 copy-start
  6.5 382.1 %all-gather.3.cloned.1.call-start = ((), (), s32[]{:S(2)}) async-start(), calls=%async_computation | async-start | bytes 14155776 | tf_op jit(solution)/shard_map/all_gather | solution.py:131
  208.2 2.2 copy-start.3
  209.7 405.9 %all-gather.5.cloned.1.call-start = ((), (), s32[]{:S(2)}) async-start(), calls=%async_computation.1 | async-start | bytes 47185920 | tf_op jit(solution)/shard_map/all_gather | solution.py:134
  394.0 270.7 %copy-start.2 = (s32[1024]{0:T(1024)S(1)}, s32[1024]{0:T(1024)}, u32[]{:S(2)}) copy-start(s32[1024]{0:T(1024)} %get-tuple-element.692) | copy-start | bytes 12292
  664.7 78.7 %copy-start.1 = (f32[12,128]{1,0:T(8,128)S(1)}, f32[12,128]{1,0:T(8,128)}, u32[]{:S(2)}) copy-start(f32[12,128]{1,0:T(8,128)} %param.21) | copy-start | bytes 18436
Sparse Core Ops, SparseCore 0:
  209.8 178.8 all-gather.2
  390.2 225.3 all-gather.4
